TPU v7x, 32 devices: a whole 2x2x4 slice. The times are simulated.
32 devices in a mesh: groups: 2 (over y), batch: 4 (over z), blk: 4 (over x, core).
Axes of the slice: x: 2, y: 2, z: 4, core: 2. Of those that a mesh axis runs over, the one named last changes fastest.
Arguments:
- queries: bfloat16 [8, 592, 1024], P(('groups', 'batch'), 'blk'), parts along dimension 0, may hold values from -12 to 12
- key_states: bfloat16 [8, 592, 1024], P(('groups', 'batch'), 'blk'), parts along dimension 0, may hold values from -6 to 6
- value_states: bfloat16 [8, 592, 1024], P(('groups', 'batch'), 'blk'), parts along dimension 0, may hold values from -6 to 6
- residual: bfloat16 [8, 592, 768], P(('groups', 'batch'), 'blk'), parts along dimension 0, may hold values from -3 to 3
- proj_weight: bfloat16 [1024, 768], P(None, 'batch'), may hold values from -0.1875 to 0.1875
- conv_weight: bfloat16 [3, 3, 768, 384], P(None, None, 'batch'), may hold values from -0.078125 to 0.078125
Outputs:
- conv_out: bfloat16 [8, 592, 384], P(('groups', 'batch'), 'blk'), parts along dimension 0
There are 2 independent parts, one for each index of `groups`. A program takes and returns all parts, laid end to end along the dimension named above; an argument that names none is the same for every part. Nothing has to cross between parts.
All inputs are finite; a program needn't handle non-finite values.
Results may differ from a plain program's by a relative error of at most 0.0085.
Values may be sent and summed in bfloat16 or wider, within the bound.
A program may use at most 64 MiB of HBM per device.

v0:
```python
import jax
import jax.numpy as jnp
from jax import lax
from jax.sharding import PartitionSpec as P

HEADS = 16
HD = 64
COLS = 74
ROWS = 2


def extended(cells, sides, width):
    for axis, dim in sides:
        count = lax.axis_size(axis)
        ends = count - 1
        head = lax.slice_in_dim(cells, 0, width, axis=dim)
        tail = lax.slice_in_dim(cells, cells.shape[dim] - width, cells.shape[dim], axis=dim)
        cells = jnp.concatenate(
            [
                lax.ppermute(tail, axis, [(i, (i + 1) % count) for i in range(ends)]),
                cells,
                lax.ppermute(head, axis, [((i + 1) % count, i) for i in range(ends)]),
            ],
            axis=dim,
        )
    return cells


def empty_state(head_count, query_rows):
    return (
        jnp.full((head_count, query_rows), -1e30, jnp.float32),
        jnp.zeros((head_count, query_rows), jnp.float32),
        jnp.zeros((head_count, query_rows, HD), jnp.float32),
    )


def absorb(carry_state, query_block, key_block, value_block):
    row_max, weight_sum, running = carry_state
    scores = jnp.einsum(
        "qhd,khd->hqk", query_block, key_block, preferred_element_type=jnp.float32
    ) * HD ** (-0.5)
    new_max = jnp.maximum(row_max, jnp.max(scores, axis=2))
    factor = jnp.exp(row_max - new_max)
    weights = jnp.exp(scores - new_max[:, :, None])
    weight_sum = weight_sum * factor + jnp.sum(weights, axis=2)
    running = running * factor[:, :, None] + jnp.einsum(
        "hqk,khd->hqd",
        weights.astype(jnp.bfloat16),
        value_block,
        preferred_element_type=jnp.float32,
    )
    return (new_max, weight_sum, running)


def finish(carry_state):
    row_max, weight_sum, running = carry_state
    mixed = running / weight_sum[:, :, None]
    head_count, query_rows = weight_sum.shape
    return mixed.transpose(1, 0, 2).reshape(query_rows, head_count * HD).astype(jnp.bfloat16)


def body(queries, key_states, value_states, residual, proj_weight, conv_weight):
    query_rows = queries[0]
    key_rows = key_states[0]
    value_rows = value_states[0]
    tok_rows = query_rows.shape[0]
    cycle_count = lax.axis_size("blk")
    local_heads = HEADS // cycle_count
    query_all, key_all, value_all = (
        lax.all_to_all(query_rows, "blk", split_axis=1, concat_axis=0, tiled=True),
        lax.all_to_all(key_rows, "blk", split_axis=1, concat_axis=0, tiled=True),
        lax.all_to_all(value_rows, "blk", split_axis=1, concat_axis=0, tiled=True),
    )
    seq_rows = tok_rows * cycle_count
    group = 1
    while cycle_count % (group * 2) == 0 and tok_rows * group * 2 <= 1024:
        group = group * 2
    block_rows = tok_rows * group
    block_count = seq_rows // block_rows
    query_blocks = query_all.reshape(block_count, block_rows, local_heads, HD)
    key_blocks = key_all.reshape(block_count, block_rows, local_heads, HD)
    value_blocks = value_all.reshape(block_count, block_rows, local_heads, HD)

    def one_block(query_block):

        def absorb_one(index, inner_state):
            return absorb(inner_state, query_block, key_blocks[index], value_blocks[index])

        return finish(
            lax.fori_loop(0, block_count, absorb_one, empty_state(local_heads, block_rows))
        )

    mixed_rows = lax.map(one_block, query_blocks).reshape(seq_rows, local_heads * HD)
    attention = lax.all_to_all(mixed_rows, "blk", split_axis=0, concat_axis=1, tiled=True)
    projected = jnp.dot(
        attention,
        lax.all_gather(proj_weight, "batch", axis=1, tiled=True),
        preferred_element_type=jnp.float32,
    )
    hidden = (residual[0].astype(jnp.float32) + projected).astype(jnp.bfloat16)
    feature_grid = hidden.reshape(ROWS, COLS, hidden.shape[1])
    rimmed = extended(feature_grid, (("blk", 0),), 1)
    padded = jnp.pad(rimmed, ((0, 0), (1, 1), (0, 0)))
    shard_piece = lax.all_gather(conv_weight, "batch", axis=2, tiled=True)
    piece_rows = shard_piece.shape[2]
    windows = []
    for row_off in range(3):
        for col_off in range(3):
            windows.append(
                padded[row_off : row_off + ROWS, col_off : col_off + COLS].reshape(
                    tok_rows, piece_rows
                )
            )
    stacked = jnp.concatenate(windows, axis=1)
    flat_weight = shard_piece.reshape(9 * piece_rows, shard_piece.shape[3])
    conv_sum = jnp.dot(stacked, flat_weight, preferred_element_type=jnp.float32)
    return conv_sum.astype(jnp.bfloat16)[None]


def solution(mesh):
    return jax.shard_map(
        body,
        mesh=mesh,
        in_specs=(
            P(("groups", "batch"), "blk", None),
            P(("groups", "batch"), "blk", None),
            P(("groups", "batch"), "blk", None),
            P(("groups", "batch"), "blk", None),
            P(None, "batch"),
            P(None, None, "batch", None),
        ),
        out_specs=P(("groups", "batch"), "blk", None),
        check_vma=False,
    )
```

profile of v0, /device:TPU:0, one launch (start us, length us, event | category | flops | bytes accessed | tf_op | source)
XLA Modules:
  0.0 159.6 jit_solution(15283503268794246920)
XLA Ops:
  8.0 1.2 all_to_all.48
  9.9 4.2 %all-to-all-start = ((bf16[148,4,256]{2,0,1:T(8,128)(2,1)}), bf16[148,4,256]{2,0,1:T(8,128)(2,1)S(1)}, u32[]{:S(2)}, u32[]{:S(2)}) async-start(bf16[148,4,256]{2,0,1:T(8,128)(2,1)} %copy.22), calls=%async_computation | async-start | bytes 622592 | tf_op jit(solution)/shard_map/all_to_all | solution.py:70
  14.3 0.8 copy.24
  15.1 5.6 %all-to-all-done = bf16[148,4,256]{2,0,1:T(8,128)(2,1)S(1)} async-done(((bf16[148,4,256]{2,0,1:T(8,128)(2,1)}), bf16[148,4,256]{2,0,1:T(8,128)(2,1)S(1)}, u32[]{:S(2)}, u32[]{:S(2)}) %all-to-all-start) | async-done | bytes 303136 | tf_op jit(solution)/shard_map/all_to_all | solution.py:70
  20.7 3.5 %all-to-all-start.1 = ((bf16[148,4,256]{2,0,1:T(8,128)(2,1)}), bf16[148,4,256]{2,0,1:T(8,128)(2,1)S(1)}, u32[]{:S(2)}, u32[]{:S(2)}) async-start(bf16[148,4,256]{2,0,1:T(8,128)(2,1)} %copy.24), calls=%async_computation.1 | async-start | bytes 622592 | tf_op jit(solution)/shard_map/all_to_all | solution.py:71
  25.0 5.6 %all-to-all-done.1 = bf16[148,4,256]{2,0,1:T(8,128)(2,1)S(1)} async-done(((bf16[148,4,256]{2,0,1:T(8,128)(2,1)}), bf16[148,4,256]{2,0,1:T(8,128)(2,1)S(1)}, u32[]{:S(2)}, u32[]{:S(2)}) %all-to-all-start.1) | async-done | bytes 303136 | tf_op jit(solution)/shard_map/all_to_all | solution.py:71
  30.6 3.5 %all-to-all-start.2 = ((bf16[148,4,256]{2,0,1:T(8,128)(2,1)}), bf16[148,4,256]{2,0,1:T(8,128)(2,1)S(1)}, u32[]{:S(2)}, u32[]{:S(2)}) async-start(bf16[148,4,256]{2,0,1:T(8,128)(2,1)} %copy.26), calls=%async_computation.2 | async-start | bytes 622592 | tf_op jit(solution)/shard_map/all_to_all | solution.py:72
  34.7 5.9 %all-to-all-done.2 = bf16[148,4,256]{2,0,1:T(8,128)(2,1)S(1)} async-done(((bf16[148,4,256]{2,0,1:T(8,128)(2,1)}), bf16[148,4,256]{2,0,1:T(8,128)(2,1)S(1)}, u32[]{:S(2)}, u32[]{:S(2)}) %all-to-all-start.2) | async-done | bytes 303136 | tf_op jit(solution)/shard_map/all_to_all | solution.py:72
  40.9 1.1 multiply_reduce_fusion
  42.0 1.0 fusion
  43.1 1.3 fusion.17
  45.1 8.9 %all_to_all.64 = bf16[4,148,256]{2,1,0:T(8,128)(2,1)S(1)} all-to-all(bf16[4,148,256]{2,1,0:T(8,128)(2,1)S(1)} %copy.29), channel_id=1, replica_groups=mesh['groups'=2,'batch'=4,'blk'=4] {'blk'}, dimensions={0} | all-to-all | bytes 606208 | tf_op jit(solution)/shard_map/all_to_all | solution.py:94
  54.3 2.2 %fusion.12 = bf16[148,768]{1,0:T(8,128)(2,1)S(1)} fusion(bf16[148,1024]{1,0:T(8,128)(2,1)S(1)} %bitcast.41, bf16[1024,768]{0,1:T(8,128)(2,1)} %all-gather.3.cloned.1.call-done, bf16[1,148,768]{2,1,0:T(8,128)(2,1)S(1)} %copy-done.2), kind=kOutput, calls=%fused_computation.12 | convolution fusion | flops 233124864 | bytes 2330624 | tf_op jit(solution)/shard_map/dot_general | solution.py:95
  56.5 1.7 %collective-permute-start = (bf16[1,74,768]{2,1,0:T(8,128)(2,1)S(1)}, bf16[1,74,768]{2,1,0:T(8,128)(2,1)S(1)}, u32[]{:S(2)}, u32[]{:S(2)}) collective-permute-start(bf16[1,74,768]{2,1,0:T(8,128)(2,1)S(1)} %get-tuple-element.60), channel_id=1, source_target_pairs={{0,1},{1,2},{2,3},{4,5},{5,6},{6,7},{8,9},{9,10},{10,11},{12,13},{... | collective-permute-start | bytes 341000 | tf_op jit(solution)/shard_map/ppermute | solution.py:20
  58.2 1.3 collective-permute-start.1
  59.6 2.0 %collective-permute-done.1 = bf16[1,74,768]{2,1,0:T(8,128)(2,1)S(1)} collective-permute-done((bf16[1,74,768]{2,1,0:T(8,128)(2,1)S(1)}, bf16[1,74,768]{2,1,0:T(8,128)(2,1)S(1)}, u32[]{:S(2)}, u32[]{:S(2)}) %collective-permute-start.1) | collective-permute-done | bytes 113696 | tf_op jit(solution)/shard_map/ppermute | solution.py:22
  62.0 0.8 reshape.82
  62.8 0.8 reshape.83
  63.5 0.8 reshape.84
  64.5 1.0 constant_dynamic-update-slice_fusion.7
  65.5 1.0 constant_dynamic-update-slice_fusion.6
  66.5 1.0 constant_dynamic-update-slice_fusion.5
  67.5 80.7 %all-gather.5.cloned.1.call-done = bf16[3,3,768,384]{3,2,1,0:T(8,128)(2,1)} async-done(((bf16[3,3,192,384]{3,2,1,0:T(8,128)(2,1)}), bf16[3,3,768,384]{3,2,1,0:T(8,128)(2,1)}) %all-gather.5.cloned.1.call-update) | async-done | bytes 5308432 | tf_op jit(solution)/shard_map/all_gather | solution.py:104
  148.3 4.5 %fusion.13 = bf16[1,148,384]{2,1,0:T(8,128)(2,1)} fusion(bf16[148,6912]{1,0:T(8,128)(2,1)S(1)} %constant_dynamic-update-slice_fusion, bf16[6912,384]{1,0:T(8,128)(2,1)} %bitcast.37), kind=kOutput, calls=%fused_computation.14 | convolution fusion | flops 785702400 | bytes 7468032 | tf_op jit(solution)/shard_map/dot_general | solution.py:116
  (42 shorter events, 5.8 us)
Async XLA Ops:
  6.5 7.6 %copy-start = (bf16[1,148,1024]{2,1,0:T(8,128)(2,1)S(1)}, bf16[1,148,1024]{2,1,0:T(8,128)(2,1)}, u32[]{:S(2)}) copy-start(bf16[1,148,1024]{2,1,0:T(8,128)(2,1)} %param.7) | copy-start | bytes 909316
  6.5 47.8 %all-gather.3.cloned.1.call-start = ((), (), s32[]{:S(2)}) async-start(), calls=%async_computation.4 | async-start | bytes 1966080 | tf_op jit(solution)/shard_map/all_gather | solution.py:97
  7.3 141.0 %all-gather.5.cloned.1.call-start = ((), (), s32[]{:S(2)}) async-start(), calls=%async_computation.5 | async-start | bytes 6635520 | tf_op jit(solution)/shard_map/all_gather | solution.py:104
  8.0 16.1 %copy-start.1 = (bf16[1,148,1024]{2,1,0:T(8,128)(2,1)S(1)}, bf16[1,148,1024]{2,1,0:T(8,128)(2,1)}, u32[]{:S(2)}) copy-start(bf16[1,148,1024]{2,1,0:T(8,128)(2,1)} %param.8) | copy-start | bytes 909316
  9.9 10.8 %all-to-all-start = ((bf16[148,4,256]{2,0,1:T(8,128)(2,1)}), bf16[148,4,256]{2,0,1:T(8,128)(2,1)S(1)}, u32[]{:S(2)}, u32[]{:S(2)}) async-start(bf16[148,4,256]{2,0,1:T(8,128)(2,1)} %copy.22), calls=%async_computation | async-start | bytes 622592 | tf_op jit(solution)/shard_map/all_to_all | solution.py:70
  20.7 10.0 %all-to-all-start.1 = ((bf16[148,4,256]{2,0,1:T(8,128)(2,1)}), bf16[148,4,256]{2,0,1:T(8,128)(2,1)S(1)}, u32[]{:S(2)}, u32[]{:S(2)}) async-start(bf16[148,4,256]{2,0,1:T(8,128)(2,1)} %copy.24), calls=%async_computation.1 | async-start | bytes 622592 | tf_op jit(solution)/shard_map/all_to_all | solution.py:71
  30.6 10.0 %all-to-all-start.2 = ((bf16[148,4,256]{2,0,1:T(8,128)(2,1)}), bf16[148,4,256]{2,0,1:T(8,128)(2,1)S(1)}, u32[]{:S(2)}, u32[]{:S(2)}) async-start(bf16[148,4,256]{2,0,1:T(8,128)(2,1)} %copy.26), calls=%async_computation.2 | async-start | bytes 622592 | tf_op jit(solution)/shard_map/all_to_all | solution.py:72
  44.4 9.9 %copy-start.2 = (bf16[1,148,768]{2,1,0:T(8,128)(2,1)S(1)}, bf16[1,148,768]{2,1,0:T(8,128)(2,1)}, u32[]{:S(2)}) copy-start(bf16[1,148,768]{2,1,0:T(8,128)(2,1)} %param.9) | copy-start | bytes 681988
  56.5 3.0 %collective-permute-start = (bf16[1,74,768]{2,1,0:T(8,128)(2,1)S(1)}, bf16[1,74,768]{2,1,0:T(8,128)(2,1)S(1)}, u32[]{:S(2)}, u32[]{:S(2)}) collective-permute-start(bf16[1,74,768]{2,1,0:T(8,128)(2,1)S(1)} %get-tuple-element.60), channel_id=1, source_target_pairs={{0,1},{1,2},{2,3},{4,5},{5,6},{6,7},{8,9},{9,10},{10,11},{12,13},{... | collective-permute-start | bytes 341000 | tf_op jit(solution)/shard_map/ppermute | solution.py:20
  58.2 3.4 %collective-permute-start.1 = (bf16[1,74,768]{2,1,0:T(8,128)(2,1)S(1)}, bf16[1,74,768]{2,1,0:T(8,128)(2,1)S(1)}, u32[]{:S(2)}, u32[]{:S(2)}) collective-permute-start(bf16[1,74,768]{2,1,0:T(8,128)(2,1)S(1)} %get-tuple-element.61), channel_id=1, source_target_pairs={{1,0},{2,1},{3,2},{5,4},{6,5},{7,6},{9,8},{10,9},{11,10},{13,12},{... | collective-permute-start | bytes 341000 | tf_op jit(solution)/shard_map/ppermute | solution.py:22
Sparse Core Ops, SparseCore 0:
  8.9 39.7 all-gather.2
  50.2 97.9 all-gather.4
where the time goes:
time: 160 us
  waiting for transfers between devices  101 us (63%)
  starting transfers between devices  14.1 us (9%)
  between operations  13.7 us (9%)
  local copies, waits for them, and re-layouts  11.2 us (7%)
  matrix products  9.04 us (6%)
  blocking collectives  8.9 us (6%)
    all_gather x1, waiting for transfers between devices, body(): shard_piece = lax.all_gather(conv_weight, 'batch', axis=2, tiled=True)  80.7 us
    all_to_all x1, blocking collectives, body(): lax.all_to_all(mixed_rows, 'blk', split_axis=0, concat_axis=1, tiled=True)  8.9 us
    all_to_all x1, waiting for transfers between devices, body(): lax.all_to_all(value_rows, 'blk', split_axis=1, concat_axis=0, tiled=True)  5.92 us
    all_to_all x1, waiting for transfers between devices, body(): lax.all_to_all(query_rows, 'blk', split_axis=1, concat_axis=0, tiled=True)  5.62 us
    all_to_all x1, waiting for transfers between devices, body(): lax.all_to_all(key_rows, 'blk', split_axis=1, concat_axis=0, tiled=True)  5.6 us
    dot_general x1, matrix products, body(): conv_sum = jnp.dot(stacked, flat_weight, preferred_element_type=jnp.float32)  4.48 us
    all_to_all x1, starting transfers between devices, body(): lax.all_to_all(query_rows, 'blk', split_axis=1, concat_axis=0, tiled=True)  4.24 us
    all_to_all x1, starting transfers between devices, body(): lax.all_to_all(value_rows, 'blk', split_axis=1, concat_axis=0, tiled=True)  3.45 us
  transfers between devices with their start and end apart: 7, of which 5 were waited for; matrix products, arithmetic and copies ran while one was open for 10% of the time, Pallas kernels for 0%

commit v1 on v0

--- a/solution.py
+++ b/solution.py
@@ -7,6 +7,12 @@
 HD = 64
 COLS = 74
 ROWS = 2
+
+
+def stacked_exchange(x, axis, split, join):
+    parts = jnp.split(x, lax.axis_size(axis), axis=split)
+    incoming = lax.all_to_all(jnp.stack(parts), axis, 0, 0)
+    return jnp.concatenate(incoming, axis=join)
 
 
 def extended(cells, sides, width):
@@ -68,7 +74,7 @@
     local_heads = HEADS // cycle_count
     query_all, key_all, value_all = (
         lax.all_to_all(query_rows, "blk", split_axis=1, concat_axis=0, tiled=True),
-        lax.all_to_all(key_rows, "blk", split_axis=1, concat_axis=0, tiled=True),
+        stacked_exchange(key_rows, "blk", 1, 0),
         lax.all_to_all(value_rows, "blk", split_axis=1, concat_axis=0, tiled=True),
     )
     seq_rows = tok_rows * cycle_count

time: 160 us -> 160 us (level)
  no operation moved by 1% of the time
where the time goes in v1:
time: 160 us
  waiting for transfers between devices  102 us (64%)
  starting transfers between devices  14.2 us (9%)
  between operations  13.7 us (9%)
  local copies, waits for them, and re-layouts  10.3 us (6%)
  blocking collectives  8.9 us (6%)
  matrix products  8.85 us (6%)
  other arithmetic  2.02 us (1%)
    all_gather x1, waiting for transfers between devices, body(): shard_piece = lax.all_gather(conv_weight, 'batch', axis=2, tiled=True)  80.9 us
    all_to_all x1, blocking collectives, body(): lax.all_to_all(mixed_rows, 'blk', split_axis=0, concat_axis=1, tiled=True)  8.9 us
    all_to_all x1, waiting for transfers between devices, stacked_exchange(): incoming = lax.all_to_all(jnp.stack(parts), axis, 0, 0)  5.92 us
    all_to_all x1, waiting for transfers between devices, body(): lax.all_to_all(value_rows, 'blk', split_axis=1, concat_axis=0, tiled=True)  5.71 us
    all_to_all x1, waiting for transfers between devices, body(): lax.all_to_all(query_rows, 'blk', split_axis=1, concat_axis=0, tiled=True)  5.61 us
    dot_general x1, matrix products, body(): conv_sum = jnp.dot(stacked, flat_weight, preferred_element_type=jnp.float32)  4.48 us
    all_to_all x1, starting transfers between devices, body(): lax.all_to_all(query_rows, 'blk', split_axis=1, concat_axis=0, tiled=True)  4.24 us
    all_to_all x1, starting transfers between devices, stacked_exchange(): incoming = lax.all_to_all(jnp.stack(parts), axis, 0, 0)  3.45 us
  transfers between devices with their start and end apart: 7, of which 5 were waited for; matrix products, arithmetic and copies ran while one was open for 10% of the time, Pallas kernels for 0%

profile of v1, /device:TPU:0, one launch (start us, length us, event | category | flops | bytes accessed | tf_op | source)
XLA Modules:
  0.0 159.6 jit_solution(10032020959119484924)
XLA Ops:
  8.0 1.2 all_to_all.40
  9.9 4.2 %all-to-all-start.1 = ((bf16[148,4,256]{2,0,1:T(8,128)(2,1)}), bf16[148,4,256]{2,0,1:T(8,128)(2,1)S(1)}, u32[]{:S(2)}, u32[]{:S(2)}) async-start(bf16[148,4,256]{2,0,1:T(8,128)(2,1)} %copy.23), calls=%async_computation.1 | async-start | bytes 622592 | tf_op jit(solution)/shard_map/all_to_all | solution.py:76
  14.3 0.8 copy.25
  15.1 5.6 %all-to-all-done.1 = bf16[148,4,256]{2,0,1:T(8,128)(2,1)S(1)} async-done(((bf16[148,4,256]{2,0,1:T(8,128)(2,1)}), bf16[148,4,256]{2,0,1:T(8,128)(2,1)S(1)}, u32[]{:S(2)}, u32[]{:S(2)}) %all-to-all-start.1) | async-done | bytes 303136 | tf_op jit(solution)/shard_map/all_to_all | solution.py:76
  20.7 3.5 %all-to-all-start.2 = ((bf16[148,4,256]{2,0,1:T(8,128)(2,1)}), bf16[148,4,256]{2,0,1:T(8,128)(2,1)S(1)}, u32[]{:S(2)}, u32[]{:S(2)}) async-start(bf16[148,4,256]{2,0,1:T(8,128)(2,1)} %copy.25), calls=%async_computation.2 | async-start | bytes 622592 | tf_op jit(solution)/shard_map/all_to_all | solution.py:78
  24.2 0.8 pad_maximum_fusion
  24.9 5.7 %all-to-all-done.2 = bf16[148,4,256]{2,0,1:T(8,128)(2,1)S(1)} async-done(((bf16[148,4,256]{2,0,1:T(8,128)(2,1)}), bf16[148,4,256]{2,0,1:T(8,128)(2,1)S(1)}, u32[]{:S(2)}, u32[]{:S(2)}) %all-to-all-start.2) | async-done | bytes 303136 | tf_op jit(solution)/shard_map/all_to_all | solution.py:78
  30.6 3.5 %all-to-all-start = ((bf16[4,148,256]{2,1,0:T(8,128)(2,1)}), bf16[4,148,256]{2,1,0:T(8,128)(2,1)S(1)}, u32[]{:S(2)}, u32[]{:S(2)}) async-start(bf16[4,148,256]{2,1,0:T(8,128)(2,1)} %pad_maximum_fusion), calls=%async_computation | async-start | bytes 622592 | tf_op jit(solution)/shard_map/all_to_all | solution.py:14
  34.7 5.9 %all-to-all-done = bf16[4,148,256]{2,1,0:T(8,128)(2,1)S(1)} async-done(((bf16[4,148,256]{2,1,0:T(8,128)(2,1)}), bf16[4,148,256]{2,1,0:T(8,128)(2,1)S(1)}, u32[]{:S(2)}, u32[]{:S(2)}) %all-to-all-start) | async-done | bytes 303136 | tf_op jit(solution)/shard_map/all_to_all | solution.py:14
  40.9 1.0 bitcast_reduce_fusion
  41.9 1.0 fusion.1
  43.0 1.3 fusion.18
  44.9 8.9 %all_to_all.53 = bf16[4,148,256]{2,1,0:T(8,128)(2,1)S(1)} all-to-all(bf16[4,148,256]{2,1,0:T(8,128)(2,1)S(1)} %copy.28), channel_id=1, replica_groups=mesh['groups'=2,'batch'=4,'blk'=4] {'blk'}, dimensions={0} | all-to-all | bytes 606208 | tf_op jit(solution)/shard_map/all_to_all | solution.py:100
  54.2 2.1 %fusion.13 = bf16[148,768]{1,0:T(8,128)(2,1)S(1)} fusion(bf16[148,1024]{1,0:T(8,128)(2,1)S(1)} %bitcast.66, bf16[1024,768]{0,1:T(8,128)(2,1)} %all-gather.3.cloned.1.call-done, bf16[1,148,768]{2,1,0:T(8,128)(2,1)S(1)} %copy-done.2), kind=kOutput, calls=%fused_computation.13 | convolution fusion | flops 233124864 | bytes 2330624 | tf_op jit(solution)/shard_map/dot_general | solution.py:101
  56.4 1.7 %collective-permute-start = (bf16[1,74,768]{2,1,0:T(8,128)(2,1)S(1)}, bf16[1,74,768]{2,1,0:T(8,128)(2,1)S(1)}, u32[]{:S(2)}, u32[]{:S(2)}) collective-permute-start(bf16[1,74,768]{2,1,0:T(8,128)(2,1)S(1)} %get-tuple-element.64), channel_id=1, source_target_pairs={{0,1},{1,2},{2,3},{4,5},{5,6},{6,7},{8,9},{9,10},{10,11},{12,13},{... | collective-permute-start | bytes 341000 | tf_op jit(solution)/shard_map/ppermute | solution.py:26
  58.1 1.3 collective-permute-start.1
  59.4 2.0 %collective-permute-done.1 = bf16[1,74,768]{2,1,0:T(8,128)(2,1)S(1)} collective-permute-done((bf16[1,74,768]{2,1,0:T(8,128)(2,1)S(1)}, bf16[1,74,768]{2,1,0:T(8,128)(2,1)S(1)}, u32[]{:S(2)}, u32[]{:S(2)}) %collective-permute-start.1) | collective-permute-done | bytes 113696 | tf_op jit(solution)/shard_map/ppermute | solution.py:28
  61.8 0.8 reshape.75
  62.6 0.7 reshape.77
  64.3 1.0 constant_dynamic-update-slice_fusion.8
  65.3 1.0 constant_dynamic-update-slice_fusion.6
  66.3 1.0 constant_dynamic-update-slice_fusion.5
  67.4 80.9 %all-gather.5.cloned.1.call-done = bf16[3,3,768,384]{3,2,1,0:T(8,128)(2,1)} async-done(((bf16[3,3,192,384]{3,2,1,0:T(8,128)(2,1)}), bf16[3,3,768,384]{3,2,1,0:T(8,128)(2,1)}) %all-gather.5.cloned.1.call-update) | async-done | bytes 5308432 | tf_op jit(solution)/shard_map/all_gather | solution.py:110
  148.3 4.5 %fusion.14 = bf16[1,148,384]{2,1,0:T(8,128)(2,1)} fusion(bf16[148,6912]{1,0:T(8,128)(2,1)S(1)} %constant_dynamic-update-slice_fusion, bf16[6912,384]{1,0:T(8,128)(2,1)} %bitcast.63), kind=kOutput, calls=%fused_computation.15 | convolution fusion | flops 785702400 | bytes 7468032 | tf_op jit(solution)/shard_map/dot_general | solution.py:122
  (42 shorter events, 5.7 us)
Async XLA Ops:
  6.5 7.6 %copy-start = (bf16[1,148,1024]{2,1,0:T(8,128)(2,1)S(1)}, bf16[1,148,1024]{2,1,0:T(8,128)(2,1)}, u32[]{:S(2)}) copy-start(bf16[1,148,1024]{2,1,0:T(8,128)(2,1)} %param.8) | copy-start | bytes 909316
  6.5 47.6 %all-gather.3.cloned.1.call-start = ((), (), s32[]{:S(2)}) async-start(), calls=%async_computation.4 | async-start | bytes 1966080 | tf_op jit(solution)/shard_map/all_gather | solution.py:103
  7.3 141.0 %all-gather.5.cloned.1.call-start = ((), (), s32[]{:S(2)}) async-start(), calls=%async_computation.5 | async-start | bytes 6635520 | tf_op jit(solution)/shard_map/all_gather | solution.py:110
  8.0 16.1 %copy-start.1 = (bf16[1,148,1024]{2,1,0:T(8,128)(2,1)S(1)}, bf16[1,148,1024]{2,1,0:T(8,128)(2,1)}, u32[]{:S(2)}) copy-start(bf16[1,148,1024]{2,1,0:T(8,128)(2,1)} %param.7) | copy-start | bytes 909316
  9.9 10.8 %all-to-all-start.1 = ((bf16[148,4,256]{2,0,1:T(8,128)(2,1)}), bf16[148,4,256]{2,0,1:T(8,128)(2,1)S(1)}, u32[]{:S(2)}, u32[]{:S(2)}) async-start(bf16[148,4,256]{2,0,1:T(8,128)(2,1)} %copy.23), calls=%async_computation.1 | async-start | bytes 622592 | tf_op jit(solution)/shard_map/all_to_all | solution.py:76
  20.7 10.0 %all-to-all-start.2 = ((bf16[148,4,256]{2,0,1:T(8,128)(2,1)}), bf16[148,4,256]{2,0,1:T(8,128)(2,1)S(1)}, u32[]{:S(2)}, u32[]{:S(2)}) async-start(bf16[148,4,256]{2,0,1:T(8,128)(2,1)} %copy.25), calls=%async_computation.2 | async-start | bytes 622592 | tf_op jit(solution)/shard_map/all_to_all | solution.py:78
  30.6 10.0 %all-to-all-start = ((bf16[4,148,256]{2,1,0:T(8,128)(2,1)}), bf16[4,148,256]{2,1,0:T(8,128)(2,1)S(1)}, u32[]{:S(2)}, u32[]{:S(2)}) async-start(bf16[4,148,256]{2,1,0:T(8,128)(2,1)} %pad_maximum_fusion), calls=%async_computation | async-start | bytes 622592 | tf_op jit(solution)/shard_map/all_to_all | solution.py:14
  44.2 9.9 %copy-start.2 = (bf16[1,148,768]{2,1,0:T(8,128)(2,1)S(1)}, bf16[1,148,768]{2,1,0:T(8,128)(2,1)}, u32[]{:S(2)}) copy-start(bf16[1,148,768]{2,1,0:T(8,128)(2,1)} %param.9) | copy-start | bytes 681988
  56.4 3.1 %collective-permute-start = (bf16[1,74,768]{2,1,0:T(8,128)(2,1)S(1)}, bf16[1,74,768]{2,1,0:T(8,128)(2,1)S(1)}, u32[]{:S(2)}, u32[]{:S(2)}) collective-permute-start(bf16[1,74,768]{2,1,0:T(8,128)(2,1)S(1)} %get-tuple-element.64), channel_id=1, source_target_pairs={{0,1},{1,2},{2,3},{4,5},{5,6},{6,7},{8,9},{9,10},{10,11},{12,13},{... | collective-permute-start | bytes 341000 | tf_op jit(solution)/shard_map/ppermute | solution.py:26
  58.1 3.4 %collective-permute-start.1 = (bf16[1,74,768]{2,1,0:T(8,128)(2,1)S(1)}, bf16[1,74,768]{2,1,0:T(8,128)(2,1)S(1)}, u32[]{:S(2)}, u32[]{:S(2)}) collective-permute-start(bf16[1,74,768]{2,1,0:T(8,128)(2,1)S(1)} %get-tuple-element.65), channel_id=1, source_target_pairs={{1,0},{2,1},{3,2},{5,4},{6,5},{7,6},{9,8},{10,9},{11,10},{13,12},{... | collective-permute-start | bytes 341000 | tf_op jit(solution)/shard_map/ppermute | solution.py:28
Sparse Core Ops, SparseCore 0:
  8.9 39.7 all-gather.2
  50.2 97.9 all-gather.4
